TPU v7x, 32 devices: a whole 2x2x4 slice. The times are simulated.
32 devices in a mesh: gx: 8 (over z, y), gy: 4 (over x, core).
Axes of the slice: x: 2, y: 2, z: 4, core: 2. Of those that a mesh axis runs over, the one named last changes fastest.
Arguments:
- three_index: bfloat16 [8, 4608, 4608], P('gx', 'gy'), as said below
- old_density: bfloat16 [4608, 4608], P('gy'), as said below
- core: float32 [4608, 4608], P('gy', 'gx'), as said below
Outputs:
- purified: bfloat16 [4608, 4608], P('gy', 'gx')
- idempotency: float32 [2], replicated
Inputs may be any that keep to these rules, and one draw needn't show every extreme that they name: Each slab three_index[P] is symmetric in its two basis indices. `old_density`: symmetric. `core`: symmetric.
All inputs are finite; a program needn't handle non-finite values.
Results may differ from a plain program's by a relative error of at most 0.015.
Values may be sent and summed in bfloat16 or wider, within the bound.
A program may use at most 128 MiB of HBM per device.

v0:
```python
import jax
import jax.numpy as jnp
from jax import lax
from jax.sharding import PartitionSpec as P

ITERS = 2


def per_device(three_index, old_density, core):
    aux_dev, rows, width = three_index.shape
    cols = core.shape[1]
    flat = three_index.reshape(aux_dev, rows * width)
    partial_value = jnp.dot(
        flat, old_density.reshape(rows * width), preferred_element_type=jnp.float32
    )
    fitted = lax.psum(partial_value, "gy")
    fitted16 = fitted.astype(jnp.bfloat16)
    coulomb = lax.psum_scatter(
        jnp.einsum("p,prc->cr", fitted16, three_index, preferred_element_type=jnp.float32).astype(
            jnp.bfloat16
        ),
        "gx",
        scatter_dimension=0,
        tiled=True,
    ).astype(jnp.float32)
    fock = core + coulomb.T
    row_start = lax.axis_index("gy") * rows
    col_start = lax.axis_index("gx") * cols
    row_ids = row_start + lax.broadcasted_iota(jnp.int32, (rows, cols), 0)
    col_ids = col_start + lax.broadcasted_iota(jnp.int32, (rows, cols), 1)
    diag_mask = (row_ids == col_ids).astype(jnp.float32)
    local_trace = jnp.sum(fock * diag_mask)
    shift = lax.psum(local_trace, ("gx", "gy")) / width
    shifted = fock - shift * diag_mask
    spread = lax.psum(jnp.sum(shifted * shifted), ("gx", "gy")) / (width * width)
    current = ((shift * diag_mask - fock) / (4.0 * jnp.sqrt(spread + 1e-06))).astype(jnp.bfloat16)
    scale = 1.0 / jnp.sqrt(jnp.float32(width))
    traces = []
    for step in range(ITERS):
        right = lax.all_gather(current, "gy", axis=0, tiled=True)
        row_panel = lax.all_gather(current, "gx", axis=1, tiled=True)
        square_full = jnp.dot(row_panel, right, preferred_element_type=jnp.float32) * scale
        square = square_full.astype(jnp.bfloat16)
        square_block = lax.all_gather(square, "gy", axis=0, tiled=True)
        cube = jnp.dot(row_panel, square_block, preferred_element_type=jnp.float32) * scale
        traces.append(jnp.sum(square_full * diag_mask))
        current = (1.5 * current.astype(jnp.float32) - 2.0 * cube).astype(jnp.bfloat16)
    totals = lax.psum(jnp.stack(traces), ("gx", "gy"))
    idempotency = 16.0 * (0.25 - totals / (width * jnp.sqrt(jnp.float32(width))))
    return (current, idempotency)


def solution(mesh):
    placed = (P("gx", "gy", None), P("gy", None), P("gy", "gx"))
    return jax.shard_map(
        per_device, mesh=mesh, in_specs=placed, out_specs=(P("gy", "gx"), P()), check_vma=False
    )
```

profile of v0, /device:TPU:0, one launch (start us, length us, event | category | flops | bytes accessed | tf_op | source)
XLA Modules:
  0.0 895.6 jit_solution(16187595499375123604)
XLA Ops:
  7.2 0.0 reduce-scatter.2.cloned.1.call-start
  7.2 19.8 %reshape.23 = bf16[5308416]{0:T(1024)(128)(2,1)} reshape(bf16[1,1152,4608]{2,1,0:T(8,128)(2,1)} %param.3) | data formatting | bytes 21233664 | tf_op jit(solution)/shard_map/reshape
  27.0 15.3 %copy.5 = bf16[1,1152,4608]{1,2,0:T(8,128)(2,1)} copy(bf16[1,1152,4608]{2,1,0:T(8,128)(2,1)} %param.3) | data formatting | bytes 21233664 | tf_op args[0]
  42.3 19.8 %reshape.24 = bf16[5308416]{0:T(1024)(128)(2,1)} reshape(bf16[1152,4608]{1,0:T(8,128)(2,1)} %param.4) | data formatting | bytes 21233664 | tf_op jit(solution)/shard_map/reshape | solution.py:14
  62.1 10.9 %fusion = f32[]{:T(128)} fusion(bf16[5308416]{0:T(1024)(128)(2,1)} %reshape.23, bf16[5308416]{0:T(1024)(128)(2,1)} %reshape.24), kind=kLoop, calls=%fused_computation.1 | loop fusion | flops 21233664 | bytes 21233668 | tf_op jit(solution)/shard_map/dot_general | solution.py:13
  72.9 9.0 %psum.28 = bf16[1]{0:T(256)(128)(2,1)} all-reduce(f32[1]{0:T(128)} %bitcast), channel_id=1, replica_groups=mesh['gx'=8,'gy'=4] {'gy'}, use_global_device_ids=true, to_apply=%region_0.0 | all-reduce | flops 1 | bytes 6 | tf_op jit(solution)/shard_map/psum | solution.py:16
  82.6 10.5 %fusion.1 = bf16[4608,1152]{1,0:T(8,128)(2,1)} fusion(bf16[1,1152,4608]{1,2,0:T(8,128)(2,1)} %copy.5, f32[]{:T(128)S(6)} %convert.13), kind=kLoop, calls=%fused_computation.3 | loop fusion | flops 15925248 | bytes 21233668 | tf_op jit(solution)/shard_map/convert_element_type | solution.py:19
  93.1 0.0 copy-start
  93.1 0.0 reduce-scatter.2.cloned.1.call-update
  93.1 0.0 all-gather.9.cloned.1.call-start
  93.2 180.8 %reduce-scatter.2.cloned.1.call-done = bf16[576,1152]{1,0:T(8,128)(2,1)} async-done(((bf16[4608,1152]{1,0:T(8,128)(2,1)}), bf16[576,1152]{1,0:T(8,128)(2,1)}) %reduce-scatter.2.cloned.1.call-update) | async-done | bytes 1327120 | tf_op jit(solution)/shard_map/reduce_scatter | solution.py:18
  274.1 0.0 copy-done
  274.1 2.8 fusion.11
  276.9 39.5 %psum.29 = f32[]{:T(128)} all-reduce(f32[]{:T(128)} %fusion.11), channel_id=1, replica_groups=mesh['gx'=8,'gy'=4] {'gx','gy'}, use_global_device_ids=true, to_apply=%region_3.0 | all-reduce | flops 1 | bytes 8 | tf_op jit(solution)/shard_map/psum | solution.py:33
  317.0 2.9 fusion.10
  319.9 40.2 %psum.30 = f32[]{:T(128)} all-reduce(f32[]{:T(128)} %fusion.10), channel_id=1, replica_groups=mesh['gx'=8,'gy'=4] {'gx','gy'}, use_global_device_ids=true, to_apply=%region_5.0 | all-reduce | flops 1 | bytes 8 | tf_op jit(solution)/shard_map/psum | solution.py:35
  360.8 3.0 fusion.14
  363.8 0.0 all-gather.9.cloned.1.call-update
  363.8 0.0 all-gather.7.cloned.1.call-start
  363.9 0.7 all-gather.7.cloned.1.call-update
  364.6 0.0 copy-start.1
  364.6 0.0 all-gather.11.cloned.1.call-start
  364.6 40.2 %all-gather.9.cloned.1.call-done = bf16[4608,576]{0,1:T(8,128)(2,1)} async-done(((bf16[1152,576]{0,1:T(8,128)(2,1)}), bf16[4608,576]{0,1:T(8,128)(2,1)}) %all-gather.9.cloned.1.call-update) | async-done | bytes 5308432 | tf_op jit(solution)/shard_map/all_gather | solution.py:40
  404.9 154.9 %all-gather.7.cloned.1.call-done = bf16[1152,4608]{0,1:T(8,128)(2,1)} async-done(((bf16[1152,576]{0,1:T(8,128)(2,1)}), bf16[1152,4608]{0,1:T(8,128)(2,1)}) %all-gather.7.cloned.1.call-update) | async-done | bytes 10616848 | tf_op jit(solution)/shard_map/all_gather | solution.py:41
  559.8 13.3 %fusion.15 = (bf16[1152,576]{0,1:T(8,128)(2,1)}, f32[1152,576]{0,1:T(8,128)}) fusion(bf16[4608,576]{0,1:T(8,128)(2,1)} %all-gather.9.cloned.1.call-done, bf16[1152,4608]{0,1:T(8,128)(2,1)} %all-gather.7.cloned.1.call-done), kind=kOutput, calls=%fused_computation.30 | convolution fusion | flops 6116622336 | bytes 19906560 | tf_op jit(solution)/shard_map/dot_general | solution.py:42
  573.1 0.0 all-gather.11.cloned.1.call-update
  573.1 0.2 all-gather.15.cloned.1.call-start
  573.4 38.9 %all-gather.11.cloned.1.call-done = bf16[4608,576]{0,1:T(8,128)(2,1)} async-done(((bf16[1152,576]{0,1:T(8,128)(2,1)}), bf16[4608,576]{0,1:T(8,128)(2,1)}) %all-gather.11.cloned.1.call-update) | async-done | bytes 5308432 | tf_op jit(solution)/shard_map/all_gather | solution.py:44
  612.2 0.0 copy-done.1
  612.2 12.9 %fusion.7 = bf16[1152,576]{0,1:T(8,128)(2,1)} fusion(bf16[4608,576]{0,1:T(8,128)(2,1)} %all-gather.11.cloned.1.call-done, bf16[1152,4608]{0,1:T(8,128)(2,1)} %all-gather.7.cloned.1.call-done, bf16[1152,576]{0,1:T(8,128)(2,1)S(1)} %copy-done.1), kind=kOutput, calls=%fused_computation.17 | convolution fusion | flops 6118612992 | bytes 18579456 | tf_op jit(solution)/shard_map/dot_general | solution.py:45
  625.1 0.0 all-gather.15.cloned.1.call-update
  625.1 0.0 all-gather.13.cloned.1.call-start
  625.2 0.5 all-gather.13.cloned.1.call-update
  625.7 0.0 all-gather.17.cloned.1.call-start
  625.7 40.3 %all-gather.15.cloned.1.call-done = bf16[4608,576]{0,1:T(8,128)(2,1)} async-done(((bf16[1152,576]{0,1:T(8,128)(2,1)}), bf16[4608,576]{0,1:T(8,128)(2,1)}) %all-gather.15.cloned.1.call-update) | async-done | bytes 5308432 | tf_op jit(solution)/shard_map/all_gather | solution.py:40
  666.0 154.8 %all-gather.13.cloned.1.call-done = bf16[1152,4608]{0,1:T(8,128)(2,1)} async-done(((bf16[1152,576]{0,1:T(8,128)(2,1)}), bf16[1152,4608]{0,1:T(8,128)(2,1)}) %all-gather.13.cloned.1.call-update) | async-done | bytes 10616848 | tf_op jit(solution)/shard_map/all_gather | solution.py:41
  820.8 0.0 copy-start.2
  820.8 14.1 %fusion.12 = (f32[]{:T(128)}, f32[]{:T(128)}, bf16[1152,576]{0,1:T(8,128)(2,1)}) fusion(f32[1152,576]{0,1:T(8,128)} %get-tuple-element.6, s32[1152]{0:T(1024)S(1)} %iota_add_fusion, s32[576]{0:T(1024)S(1)} %iota_add_fusion.1, bf16[4608,576]{0,1:T(8,128)(2,1)} %all-gather.15.cloned.1.call-done, bf16[1152,4608]{0,1:T(8,128)(2,1)} %all-gather.13.cloned.1.call-done), kind=kOutput, calls=%fused_computation.22 | convolution fusion | flops 6119940096 | bytes 19913480 | tf_op jit(solution)/shard_map/dot_general | solution.py:42
  834.9 0.0 all-gather.17.cloned.1.call-update
  834.9 1.4 pad_maximum_fusion
  836.3 39.1 %psum.31 = f32[2]{0:T(128)S(1)} all-reduce(f32[2]{0:T(128)S(1)} %pad_maximum_fusion), channel_id=1, replica_groups=mesh['gx'=8,'gy'=4] {'gx','gy'}, use_global_device_ids=true, to_apply=%region_8.0 | all-reduce | flops 2 | bytes 16 | tf_op jit(solution)/shard_map/psum | solution.py:48
  875.4 0.5 subtract_multiply_fusion
  875.9 0.0 all-gather.17.cloned.1.call-done
  875.9 0.0 copy-done.2
  875.9 12.9 %fusion.6 = bf16[1152,576]{0,1:T(8,128)(2,1)} fusion(bf16[4608,576]{0,1:T(8,128)(2,1)} %all-gather.17.cloned.1.call-done, bf16[1152,4608]{0,1:T(8,128)(2,1)} %all-gather.13.cloned.1.call-done, bf16[1152,576]{0,1:T(8,128)(2,1)S(1)} %copy-done.2), kind=kOutput, calls=%fused_computation.16 | convolution fusion | flops 6118612992 | bytes 18579456 | tf_op jit(solution)/shard_map/dot_general | solution.py:45
  (2 shorter events, 0.0 us)
Async XLA Ops:
  7.2 266.9 %reduce-scatter.2.cloned.1.call-start = ((), (), s32[]{:S(2)}) async-start(), calls=%async_computation.1 | async-start | bytes 11943936 | tf_op jit(solution)/shard_map/reduce_scatter | solution.py:18
  93.1 181.0 %copy-start = (f32[1152,576]{0,1:T(8,128)S(1)}, f32[1152,576]{0,1:T(8,128)}, u32[]{:S(2)}) copy-start(f32[1152,576]{0,1:T(8,128)} %param.5) | copy-start | bytes 7962628
  93.1 311.7 %all-gather.9.cloned.1.call-start = ((), (), s32[]{:S(2)}) async-start(), calls=%async_computation.3 | async-start | bytes 6635520 | tf_op jit(solution)/shard_map/all_gather | solution.py:40
  363.8 196.0 %all-gather.7.cloned.1.call-start = ((), (), s32[]{:S(2)}) async-start(), calls=%async_computation.2 | async-start | bytes 11943936 | tf_op jit(solution)/shard_map/all_gather | solution.py:41
  364.6 247.7 %copy-start.1 = (bf16[1152,576]{0,1:T(8,128)(2,1)S(1)}, bf16[1152,576]{0,1:T(8,128)(2,1)}, u32[]{:S(2)}) copy-start(bf16[1152,576]{0,1:T(8,128)(2,1)} %fusion.14) | copy-start | bytes 3981316
  364.6 247.6 %all-gather.11.cloned.1.call-start = ((), (), s32[]{:S(2)}) async-start(), calls=%async_computation.4 | async-start | bytes 6635520 | tf_op jit(solution)/shard_map/all_gather | solution.py:44
  573.1 92.9 %all-gather.15.cloned.1.call-start = ((), (), s32[]{:S(2)}) async-start(), calls=%async_computation.6 | async-start | bytes 6635520 | tf_op jit(solution)/shard_map/all_gather | solution.py:40
  625.1 195.7 %all-gather.13.cloned.1.call-start = ((), (), s32[]{:S(2)}) async-start(), calls=%async_computation.5 | async-start | bytes 11943936 | tf_op jit(solution)/shard_map/all_gather | solution.py:41
  625.7 250.2 %all-gather.17.cloned.1.call-start = ((), (), s32[]{:S(2)}) async-start(), calls=%async_computation.7 | async-start | bytes 6635520 | tf_op jit(solution)/shard_map/all_gather | solution.py:44
  820.8 55.1 %copy-start.2 = (bf16[1152,576]{0,1:T(8,128)(2,1)S(1)}, bf16[1152,576]{0,1:T(8,128)(2,1)}, u32[]{:S(2)}) copy-start(bf16[1152,576]{0,1:T(8,128)(2,1)} %fusion.7) | copy-start | bytes 3981316
Sparse Core Ops, SparseCore 0:
  93.3 180.7 reduce-scatter.1
  363.9 40.8 all-gather.8
  407.6 152.1 all-gather.6
  573.3 38.9 all-gather.10
  625.2 40.7 all-gather.14
  668.6 152.1 all-gather.12
  835.0 39.4 all-gather.16
where the time goes:
time: 897 us; the launch traced here: 896 us
  waiting for transfers between devices  611 us (68%)
  blocking collectives  128 us (14%)
  local copies, waits for them, and re-layouts  54.9 us (6%)
  matrix products  53.1 us (6%)
  other arithmetic  32 us (4%)
  between operations  16.2 us (2%)
    all_gather x2, waiting for transfers between devices, per_device(): row_panel = lax.all_gather(current, 'gx', axis=1, tiled=True)  310 us
    reduce_scatter x1, waiting for transfers between devices, per_device(): lax.psum_scatter(jnp.einsum('p,prc->cr', fitted16, three_index, preferred...  181 us
    all_gather x2, waiting for transfers between devices, per_device(): right = lax.all_gather(current, 'gy', axis=0, tiled=True)  80.5 us
    psum x1, blocking collectives, per_device(): lax.psum(jnp.sum(shifted * shifted), ('gx', 'gy')) / (width * width)  40.2 us
    psum x1, blocking collectives, per_device(): shift = lax.psum(local_trace, ('gx', 'gy')) / width  39.5 us
    psum x1, blocking collectives, per_device(): totals = lax.psum(jnp.stack(traces), ('gx', 'gy'))  39.1 us
    all_gather x2, waiting for transfers between devices, per_device(): square_block = lax.all_gather(square, 'gy', axis=0, tiled=True)  38.9 us
    dot_general x2, matrix products, per_device(): jnp.dot(row_panel, right, preferred_element_type=jnp.float32) * scale  27.4 us
  transfers between devices with their start and end apart: 7, of which 6 were waited for; matrix products, arithmetic and copies ran while one was open for 0% of the time, Pallas kernels for 0%

commit v1 on v0

--- a/solution.py
+++ b/solution.py
@@ -37,7 +37,14 @@
     scale = 1.0 / jnp.sqrt(jnp.float32(width))
     traces = []
     for step in range(ITERS):
-        right = lax.all_gather(current, "gy", axis=0, tiled=True)
+        ring = [current]
+        for hop in range(3):
+            ring.append(lax.ppermute(ring[-1], "gy", [(dev, (dev + 1) % 4) for dev in range(4)]))
+        right = jnp.roll(
+            jnp.concatenate(ring[::-1], axis=0),
+            (lax.axis_index("gy") + 1) * ring[0].shape[0],
+            axis=0,
+        )
         row_panel = lax.all_gather(current, "gx", axis=1, tiled=True)
         square_full = jnp.dot(row_panel, right, preferred_element_type=jnp.float32) * scale
         square = square_full.astype(jnp.bfloat16)

time: 897 us -> 834 us (0.930)
  waiting for transfers between devices: 611 us -> 523 us
  matrix products: 53.1 us -> 77.4 us
    all_gather x2, waiting for transfers between devices: 310 us -> 199 us  [per_device(): row_panel = lax.all_gather(current, 'gx', axis=1, tiled=True)]
    ppermute x0 -> x6, waiting for transfers between devices: none -> 104 us  [per_device(): lax.ppermute(ring[-1], 'gy', [(dev, (dev + 1) % 4) for dev in range(4)])]
    all_gather x2 -> x0, waiting for transfers between devices: 80.5 us -> none  [per_device(): right = lax.all_gather(current, 'gy', axis=0, tiled=True)]
    dot_general x2, matrix products: 27.4 us -> 51.6 us  [per_device(): jnp.dot(row_panel, right, preferred_element_type=jnp.float32) * scale]
  transfers between devices with their start and end apart: 7 -> 11, of which waited for: 6 -> 10; matrix products, arithmetic and copies ran while one was open for 0% -> 0% of each run, Pallas kernels for 0% -> 0%
where the time goes in v1:
time: 834 us; the launch traced here: 833 us
  waiting for transfers between devices  523 us (63%)
  blocking collectives  128 us (15%)
  matrix products  77.4 us (9%)
  local copies, waits for them, and re-layouts  56 us (7%)
  other arithmetic  32 us (4%)
  between operations  15.8 us (2%)
    all_gather x2, waiting for transfers between devices, per_device(): row_panel = lax.all_gather(current, 'gx', axis=1, tiled=True)  199 us
    reduce_scatter x1, waiting for transfers between devices, per_device(): lax.psum_scatter(jnp.einsum('p,prc->cr', fitted16, three_index, preferred...  181 us
    ppermute x6, waiting for transfers between devices, per_device(): lax.ppermute(ring[-1], 'gy', [(dev, (dev + 1) % 4) for dev in range(4)])  104 us
    dot_general x2, matrix products, per_device(): jnp.dot(row_panel, right, preferred_element_type=jnp.float32) * scale  51.6 us
    psum x1, blocking collectives, per_device(): lax.psum(jnp.sum(shifted * shifted), ('gx', 'gy')) / (width * width)  40.2 us
    psum x1, blocking collectives, per_device(): shift = lax.psum(local_trace, ('gx', 'gy')) / width  39.5 us
    psum x1, blocking collectives, per_device(): totals = lax.psum(jnp.stack(traces), ('gx', 'gy'))  39.1 us
    all_gather x2, waiting for transfers between devices, per_device(): square_block = lax.all_gather(square, 'gy', axis=0, tiled=True)  39 us
  transfers between devices with their start and end apart: 11, of which 10 were waited for; matrix products, arithmetic and copies ran while one was open for 0% of the time, Pallas kernels for 0%

profile of v1, /device:TPU:0, one launch (start us, length us, event | category | flops | bytes accessed | tf_op | source)
XLA Modules:
  0.0 832.6 jit_solution(9731788551176552678)
XLA Ops:
  7.2 0.0 reduce-scatter.2.cloned.1.call-start
  7.2 19.8 %reshape.23 = bf16[5308416]{0:T(1024)(128)(2,1)} reshape(bf16[1,1152,4608]{2,1,0:T(8,128)(2,1)} %param.5) | data formatting | bytes 21233664 | tf_op jit(solution)/shard_map/reshape
  27.0 15.3 %copy.5 = bf16[1,1152,4608]{1,2,0:T(8,128)(2,1)} copy(bf16[1,1152,4608]{2,1,0:T(8,128)(2,1)} %param.5) | data formatting | bytes 21233664 | tf_op args[0]
  42.3 19.8 %reshape.24 = bf16[5308416]{0:T(1024)(128)(2,1)} reshape(bf16[1152,4608]{1,0:T(8,128)(2,1)} %param.6) | data formatting | bytes 21233664 | tf_op jit(solution)/shard_map/reshape | solution.py:14
  62.1 10.9 %fusion = f32[]{:T(128)} fusion(bf16[5308416]{0:T(1024)(128)(2,1)} %reshape.23, bf16[5308416]{0:T(1024)(128)(2,1)} %reshape.24), kind=kLoop, calls=%fused_computation.1 | loop fusion | flops 21233664 | bytes 21233668 | tf_op jit(solution)/shard_map/dot_general | solution.py:13
  72.9 9.0 %psum.28 = bf16[1]{0:T(256)(128)(2,1)} all-reduce(f32[1]{0:T(128)} %bitcast), channel_id=1, replica_groups=mesh['gx'=8,'gy'=4] {'gy'}, use_global_device_ids=true, to_apply=%region_0.0 | all-reduce | flops 1 | bytes 6 | tf_op jit(solution)/shard_map/psum | solution.py:16
  82.6 10.5 %fusion.1 = bf16[4608,1152]{1,0:T(8,128)(2,1)} fusion(bf16[1,1152,4608]{1,2,0:T(8,128)(2,1)} %copy.5, f32[]{:T(128)S(6)} %convert.13), kind=kLoop, calls=%fused_computation.3 | loop fusion | flops 15925248 | bytes 21233668 | tf_op jit(solution)/shard_map/convert_element_type | solution.py:19
  93.1 0.0 copy-start
  93.1 0.0 reduce-scatter.2.cloned.1.call-update
  93.1 0.0 all-gather.5.cloned.1.call-start
  93.2 180.8 %reduce-scatter.2.cloned.1.call-done = bf16[576,1152]{1,0:T(8,128)(2,1)} async-done(((bf16[4608,1152]{1,0:T(8,128)(2,1)}), bf16[576,1152]{1,0:T(8,128)(2,1)}) %reduce-scatter.2.cloned.1.call-update) | async-done | bytes 1327120 | tf_op jit(solution)/shard_map/reduce_scatter | solution.py:18
  274.1 0.0 copy-done
  274.1 2.8 fusion.37
  276.9 39.5 %psum.29 = f32[]{:T(128)} all-reduce(f32[]{:T(128)} %fusion.37), channel_id=1, replica_groups=mesh['gx'=8,'gy'=4] {'gx','gy'}, use_global_device_ids=true, to_apply=%region_3.0 | all-reduce | flops 1 | bytes 8 | tf_op jit(solution)/shard_map/psum | solution.py:33
  317.0 2.9 fusion.36
  319.9 40.2 %psum.30 = f32[]{:T(128)} all-reduce(f32[]{:T(128)} %fusion.36), channel_id=1, replica_groups=mesh['gx'=8,'gy'=4] {'gx','gy'}, use_global_device_ids=true, to_apply=%region_5.0 | all-reduce | flops 1 | bytes 8 | tf_op jit(solution)/shard_map/psum | solution.py:35
  360.8 3.0 fusion.40
  363.8 0.0 all-gather.5.cloned.1.call-update
  363.8 0.0 all-gather.7.cloned.1.call-start
  363.9 0.1 collective-permute-start
  364.0 17.4 %collective-permute-done = bf16[1152,576]{0,1:T(8,128)(2,1)S(1)} collective-permute-done((bf16[1152,576]{0,1:T(8,128)(2,1)}, bf16[1152,576]{0,1:T(8,128)(2,1)S(1)}, u32[]{:S(2)}, u32[]{:S(2)}) %collective-permute-start) | collective-permute-done | bytes 1327136 | tf_op jit(solution)/shard_map/ppermute | solution.py:42
  381.4 0.0 collective-permute-start.1
  381.4 17.3 %collective-permute-done.1 = bf16[1152,576]{0,1:T(8,128)(2,1)} collective-permute-done((bf16[1152,576]{0,1:T(8,128)(2,1)S(1)}, bf16[1152,576]{0,1:T(8,128)(2,1)}, u32[]{:S(2)}, u32[]{:S(2)}) %collective-permute-start.1) | collective-permute-done | bytes 1327136 | tf_op jit(solution)/shard_map/ppermute | solution.py:42
  398.7 0.0 collective-permute-start.2
  398.7 0.0 copy-start.1
  398.7 17.5 %collective-permute-done.2 = bf16[1152,576]{0,1:T(8,128)(2,1)} collective-permute-done((bf16[1152,576]{0,1:T(8,128)(2,1)}, bf16[1152,576]{0,1:T(8,128)(2,1)}, u32[]{:S(2)}, u32[]{:S(2)}) %collective-permute-start.2) | collective-permute-done | bytes 1327136 | tf_op jit(solution)/shard_map/ppermute | solution.py:42
  416.2 100.0 %all-gather.5.cloned.1.call-done = bf16[1152,4608]{0,1:T(8,128)(2,1)} async-done(((bf16[1152,576]{0,1:T(8,128)(2,1)}), bf16[1152,4608]{0,1:T(8,128)(2,1)}) %all-gather.5.cloned.1.call-update) | async-done | bytes 10616848 | tf_op jit(solution)/shard_map/all_gather | solution.py:48
  516.2 25.3 %fusion.45 = (bf16[1152,576]{0,1:T(8,128)(2,1)}, f32[1152,576]{0,1:T(8,128)}) fusion(bf16[1152,4608]{0,1:T(8,128)(2,1)} %all-gather.5.cloned.1.call-done, s32[]{:T(128)S(6)} %select_n.13, bf16[1152,576]{0,1:T(8,128)(2,1)} %collective-permute-done.2, bf16[1152,576]{0,1:T(8,128)(2,1)} %collective-permute-done.1, ...), kind=kOutput, calls=%fused_computation.66 | convolution fusion | flops 6159089664 | bytes 19906564 | tf_op jit(solution)/shard_map/dot_general | solution.py:49
  541.5 0.0 all-gather.7.cloned.1.call-update
  541.5 0.0 all-gather.9.cloned.1.call-start
  541.6 39.0 %all-gather.7.cloned.1.call-done = bf16[4608,576]{0,1:T(8,128)(2,1)} async-done(((bf16[1152,576]{0,1:T(8,128)(2,1)}), bf16[4608,576]{0,1:T(8,128)(2,1)}) %all-gather.7.cloned.1.call-update) | async-done | bytes 5308432 | tf_op jit(solution)/shard_map/all_gather | solution.py:51
  580.6 0.0 copy-done.1
  580.6 12.9 %fusion.33 = bf16[1152,576]{0,1:T(8,128)(2,1)} fusion(bf16[4608,576]{0,1:T(8,128)(2,1)} %all-gather.7.cloned.1.call-done, bf16[1152,4608]{0,1:T(8,128)(2,1)} %all-gather.5.cloned.1.call-done, bf16[1152,576]{0,1:T(8,128)(2,1)S(1)} %copy-done.1), kind=kOutput, calls=%fused_computation.49 | convolution fusion | flops 6118612992 | bytes 18579456 | tf_op jit(solution)/shard_map/dot_general | solution.py:52
  593.5 0.0 all-gather.9.cloned.1.call-update
  593.5 0.0 all-gather.11.cloned.1.call-start
  593.5 0.3 collective-permute-start.3
  593.8 17.2 %collective-permute-done.3 = bf16[1152,576]{0,1:T(8,128)(2,1)S(1)} collective-permute-done((bf16[1152,576]{0,1:T(8,128)(2,1)}, bf16[1152,576]{0,1:T(8,128)(2,1)S(1)}, u32[]{:S(2)}, u32[]{:S(2)}) %collective-permute-start.3) | collective-permute-done | bytes 1327136 | tf_op jit(solution)/shard_map/ppermute | solution.py:42
  611.0 0.0 collective-permute-start.4
  611.0 17.2 %collective-permute-done.4 = bf16[1152,576]{0,1:T(8,128)(2,1)S(1)} collective-permute-done((bf16[1152,576]{0,1:T(8,128)(2,1)S(1)}, bf16[1152,576]{0,1:T(8,128)(2,1)S(1)}, u32[]{:S(2)}, u32[]{:S(2)}) %collective-permute-start.4) | collective-permute-done | bytes 1327136 | tf_op jit(solution)/shard_map/ppermute | solution.py:42
  628.2 0.0 copy-start.3
  628.2 1.1 copy-done.3
  629.3 0.0 collective-permute-start.5
  629.3 17.3 %collective-permute-done.5 = bf16[1152,576]{0,1:T(8,128)(2,1)} collective-permute-done((bf16[1152,576]{0,1:T(8,128)(2,1)S(1)}, bf16[1152,576]{0,1:T(8,128)(2,1)}, u32[]{:S(2)}, u32[]{:S(2)}) %collective-permute-start.5) | collective-permute-done | bytes 1327136 | tf_op jit(solution)/shard_map/ppermute | solution.py:42
  646.7 99.1 %all-gather.9.cloned.1.call-done = bf16[1152,4608]{0,1:T(8,128)(2,1)} async-done(((bf16[1152,576]{0,1:T(8,128)(2,1)}), bf16[1152,4608]{0,1:T(8,128)(2,1)}) %all-gather.9.cloned.1.call-update) | async-done | bytes 10616848 | tf_op jit(solution)/shard_map/all_gather | solution.py:48
  745.8 0.0 copy-start.2
  745.8 26.4 %fusion.38 = (f32[]{:T(128)}, f32[]{:T(128)}, bf16[1152,576]{0,1:T(8,128)(2,1)}) fusion(f32[1152,576]{0,1:T(8,128)} %get-tuple-element.7, s32[1152]{0:T(1024)S(1)} %iota_add_fusion, s32[576]{0:T(1024)S(1)} %iota_add_fusion.1, bf16[1152,4608]{0,1:T(8,128)(2,1)} %all-gather.9.cloned.1.call-done, s32[]{:T(128)S(6)} %select_n.13, ...), kind=kOutput, calls=%fused_computation.54 | convolution fusion | flops 6162407424 | bytes 19913484 | tf_op jit(solution)/shard_map/dot_general | solution.py:49
  772.1 0.0 all-gather.11.cloned.1.call-update
  772.2 1.4 pad_maximum_fusion
  773.6 39.1 %psum.31 = f32[2]{0:T(128)S(1)} all-reduce(f32[2]{0:T(128)S(1)} %pad_maximum_fusion), channel_id=1, replica_groups=mesh['gx'=8,'gy'=4] {'gx','gy'}, use_global_device_ids=true, to_apply=%region_8.10 | all-reduce | flops 2 | bytes 16 | tf_op jit(solution)/shard_map/psum | solution.py:55
  812.7 0.5 subtract_multiply_fusion
  813.2 0.0 all-gather.11.cloned.1.call-done
  813.2 0.0 copy-done.2
  813.2 12.9 %fusion.32 = bf16[1152,576]{0,1:T(8,128)(2,1)} fusion(bf16[4608,576]{0,1:T(8,128)(2,1)} %all-gather.11.cloned.1.call-done, bf16[1152,4608]{0,1:T(8,128)(2,1)} %all-gather.9.cloned.1.call-done, bf16[1152,576]{0,1:T(8,128)(2,1)S(1)} %copy-done.2), kind=kOutput, calls=%fused_computation.48 | convolution fusion | flops 6118612992 | bytes 18579456 | tf_op jit(solution)/shard_map/dot_general | solution.py:52
  (2 shorter events, 0.0 us)
Async XLA Ops:
  7.2 266.9 %reduce-scatter.2.cloned.1.call-start = ((), (), s32[]{:S(2)}) async-start(), calls=%async_computation.1 | async-start | bytes 11943936 | tf_op jit(solution)/shard_map/reduce_scatter | solution.py:18
  93.1 181.0 %copy-start = (f32[1152,576]{0,1:T(8,128)S(1)}, f32[1152,576]{0,1:T(8,128)}, u32[]{:S(2)}) copy-start(f32[1152,576]{0,1:T(8,128)} %param.7) | copy-start | bytes 7962628
  93.1 423.1 %all-gather.5.cloned.1.call-start = ((), (), s32[]{:S(2)}) async-start(), calls=%async_computation.2 | async-start | bytes 11943936 | tf_op jit(solution)/shard_map/all_gather | solution.py:48
  363.8 216.8 %all-gather.7.cloned.1.call-start = ((), (), s32[]{:S(2)}) async-start(), calls=%async_computation.3 | async-start | bytes 6635520 | tf_op jit(solution)/shard_map/all_gather | solution.py:51
  363.9 17.5 %collective-permute-start = (bf16[1152,576]{0,1:T(8,128)(2,1)}, bf16[1152,576]{0,1:T(8,128)(2,1)S(1)}, u32[]{:S(2)}, u32[]{:S(2)}) collective-permute-start(bf16[1152,576]{0,1:T(8,128)(2,1)} %fusion.40), channel_id=1, source_target_pairs={{0,1},{1,2},{2,3},{3,0},{4,5},{5,6},{6,7},{7,4},{8,9},{9,10},{10,1... | collective-permute-start | bytes 3981320 | tf_op jit(solution)/shard_map/ppermute | solution.py:42
  381.4 17.3 %collective-permute-start.1 = (bf16[1152,576]{0,1:T(8,128)(2,1)S(1)}, bf16[1152,576]{0,1:T(8,128)(2,1)}, u32[]{:S(2)}, u32[]{:S(2)}) collective-permute-start(bf16[1152,576]{0,1:T(8,128)(2,1)S(1)} %collective-permute-done), channel_id=1, source_target_pairs={{0,1},{1,2},{2,3},{3,0},{4,5},{5,6},{6,7},{7,4},{8,9},{9,10},{10,1... | collective-permute-start | bytes 3981320 | tf_op jit(solution)/shard_map/ppermute | solution.py:42
  398.7 17.5 %collective-permute-start.2 = (bf16[1152,576]{0,1:T(8,128)(2,1)}, bf16[1152,576]{0,1:T(8,128)(2,1)}, u32[]{:S(2)}, u32[]{:S(2)}) collective-permute-start(bf16[1152,576]{0,1:T(8,128)(2,1)} %collective-permute-done.1), channel_id=1, source_target_pairs={{0,1},{1,2},{2,3},{3,0},{4,5},{5,6},{6,7},{7,4},{8,9},{9,10},{10,1... | collective-permute-start | bytes 3981320 | tf_op jit(solution)/shard_map/ppermute | solution.py:42
  398.7 181.9 %copy-start.1 = (bf16[1152,576]{0,1:T(8,128)(2,1)S(1)}, bf16[1152,576]{0,1:T(8,128)(2,1)}, u32[]{:S(2)}) copy-start(bf16[1152,576]{0,1:T(8,128)(2,1)} %fusion.40) | copy-start | bytes 3981316
  541.5 204.2 %all-gather.9.cloned.1.call-start = ((), (), s32[]{:S(2)}) async-start(), calls=%async_computation.4 | async-start | bytes 11943936 | tf_op jit(solution)/shard_map/all_gather | solution.py:48
  593.5 219.7 %all-gather.11.cloned.1.call-start = ((), (), s32[]{:S(2)}) async-start(), calls=%async_computation.5 | async-start | bytes 6635520 | tf_op jit(solution)/shard_map/all_gather | solution.py:51
  593.5 17.5 %collective-permute-start.3 = (bf16[1152,576]{0,1:T(8,128)(2,1)}, bf16[1152,576]{0,1:T(8,128)(2,1)S(1)}, u32[]{:S(2)}, u32[]{:S(2)}) collective-permute-start(bf16[1152,576]{0,1:T(8,128)(2,1)} %fusion.33), channel_id=1, source_target_pairs={{0,1},{1,2},{2,3},{3,0},{4,5},{5,6},{6,7},{7,4},{8,9},{9,10},{10,1... | collective-permute-start | bytes 3981320 | tf_op jit(solution)/shard_map/ppermute | solution.py:42
  611.0 17.2 %collective-permute-start.4 = (bf16[1152,576]{0,1:T(8,128)(2,1)S(1)}, bf16[1152,576]{0,1:T(8,128)(2,1)S(1)}, u32[]{:S(2)}, u32[]{:S(2)}) collective-permute-start(bf16[1152,576]{0,1:T(8,128)(2,1)S(1)} %collective-permute-done.3), channel_id=1, source_target_pairs={{0,1},{1,2},{2,3},{3,0},{4,5},{5,6},{6,7},{7,4},{8,9},{9,10},{10,1... | collective-permute-start | bytes 3981320 | tf_op jit(solution)/shard_map/ppermute | solution.py:42
  628.2 1.1 copy-start.3
  629.3 17.3 %collective-permute-start.5 = (bf16[1152,576]{0,1:T(8,128)(2,1)S(1)}, bf16[1152,576]{0,1:T(8,128)(2,1)}, u32[]{:S(2)}, u32[]{:S(2)}) collective-permute-start(bf16[1152,576]{0,1:T(8,128)(2,1)S(1)} %collective-permute-done.4), channel_id=1, source_target_pairs={{0,1},{1,2},{2,3},{3,0},{4,5},{5,6},{6,7},{7,4},{8,9},{9,10},{10,1... | collective-permute-start | bytes 3981320 | tf_op jit(solution)/shard_map/ppermute | solution.py:42
  745.8 67.4 %copy-start.2 = (bf16[1152,576]{0,1:T(8,128)(2,1)S(1)}, bf16[1152,576]{0,1:T(8,128)(2,1)}, u32[]{:S(2)}) copy-start(bf16[1152,576]{0,1:T(8,128)(2,1)} %fusion.33) | copy-start | bytes 3981316
Sparse Core Ops, SparseCore 0:
  93.3 180.7 reduce-scatter.1
  364.0 152.2 all-gather.4
  541.7 38.8 all-gather.6
  593.6 152.1 all-gather.8
  772.3 39.4 all-gather.10
